TPU v7x, 32 devices: a whole 2x2x4 slice. The times are simulated.
32 devices in a mesh: rep: 4 (over x, core), shard: 8 (over z, y).
Axes of the slice: x: 2, y: 2, z: 4, core: 2. Of those that a mesh axis runs over, the one named last changes fastest.
Arguments:
- images: bfloat16 [32, 256, 1152], P(('rep', 'shard')), may hold values from -6 to 6
- cotangent: bfloat16 [32, 256, 1152], P(('rep', 'shard')), may hold values from -6 to 6
- w_qkv: bfloat16 [1152, 3456], P('shard'), may hold values from -2 to 2
- w_out: bfloat16 [1152, 1152], P('shard'), may hold values from -0.75 to 0.75
- w_up: bfloat16 [1152, 4304], P('shard'), may hold values from -0.1875 to 0.1875
- w_down: bfloat16 [1152, 4304], P('shard'), may hold values from -0.125 to 0.125
- vectors: bfloat16 [1152, 8], P('shard'), may hold values from -3 to 3, as said below
- up_bias: bfloat16 [4304], replicated, may hold values from -3 to 3
Outputs:
- outputs: bfloat16 [32, 256, 1152], P(('rep', 'shard'))
- input_grad: bfloat16 [32, 256, 1152], P(('rep', 'shard'))
- qkv_grad: float32 [1152, 3456], P('shard')
- out_grad: float32 [1152, 1152], P('shard')
- up_grad: float32 [1152, 4304], P('shard')
- down_grad: float32 [1152, 4304], P('shard')
- vectors_grad: float32 [1152, 8], P('shard')
- up_bias_grad: float32 [4304], replicated
Inputs may be any that keep to these rules, and one draw needn't show every extreme that they name: `vectors`: columns 0 and 5 (the norms' gains) are positive; the other columns have either sign.
All inputs are finite; a program needn't handle non-finite values.
Results may differ from a plain program's by a relative error of at most 0.014.
Values may be sent and summed in bfloat16 or wider, within the bound.
A program may use at most 256 MiB of HBM per device.

v0:
```python
import math
import jax
import jax.numpy as jnp
from jax import lax
from jax.sharding import PartitionSpec as P

HEAD_DIM = 72
EPSILON = 1e-06
GELU_COEF = 0.044715
ROOT_TWO_PI = math.sqrt(2.0 / math.pi)
F32 = jnp.float32
BF16 = jnp.bfloat16


def dot(a, b, ca, cb):
    return lax.dot_general(a, b, (((ca,), (cb,)), ((), ())), preferred_element_type=F32)


def batched(pattern, left_op, right_op):
    return jnp.einsum(pattern, left_op, right_op, preferred_element_type=F32)


def norm_rows(hidden):
    row_mean = jnp.mean(hidden, axis=-1, keepdims=True)
    centered = hidden - row_mean
    variance = jnp.mean(centered * centered, axis=-1, keepdims=True)
    inv_std = lax.rsqrt(variance + EPSILON)
    return (centered * inv_std, inv_std)


def norm_back(grad_normed, normed, inv_std):
    mean_grad = jnp.mean(grad_normed, axis=-1, keepdims=True)
    mean_proj = jnp.mean(grad_normed * normed, axis=-1, keepdims=True)
    return inv_std * (grad_normed - mean_grad - normed * mean_proj)


def gelu_parts(u):
    t = jnp.tanh(ROOT_TWO_PI * (u + GELU_COEF * u * u * u))
    act = 0.5 * u * (1.0 + t)
    der = 0.5 * (1.0 + t) + 0.5 * u * (1.0 - t * t) * ROOT_TWO_PI * (1.0 + 3.0 * GELU_COEF * u * u)
    return (act, der)


def gather_rep(a):
    return lax.all_gather(a, "rep", axis=0, tiled=True)


def scatter_rep(a):
    return lax.psum_scatter(a.astype(BF16), "rep", scatter_dimension=0, tiled=True).astype(F32)


def per_device(reps, images, cotangent, w_qkv, w_out, w_up, w_down, vectors, up_bias):
    r = lax.axis_index("rep")
    batch, seq, width = images.shape
    rows = w_qkv.shape[0]
    quarter = width // reps
    ffq = w_up.shape[1] // reps
    heads = quarter // HEAD_DIM

    def take(w, start, size):
        return lax.dynamic_slice_in_dim(w, start, size, 1)

    part = jnp.concatenate(
        [take(w_qkv, t * width + r * quarter, quarter) for t in range(3)], axis=1
    )
    mine_up = take(w_up, r * ffq, ffq)
    mine_down = take(w_down, r * ffq, ffq)
    wq = lax.all_gather(part, "shard", axis=0, tiled=True)
    wo = lax.all_gather(w_out, "shard", axis=0, tiled=True)
    wu = lax.all_gather(mine_up, "shard", axis=0, tiled=True)
    wd = lax.all_gather(mine_down, "shard", axis=0, tiled=True)
    params = lax.all_gather(vectors, "shard", axis=0, tiled=True).astype(F32)
    wo = lax.dynamic_slice_in_dim(wo, r * quarter, quarter, 0)
    bias_up = lax.dynamic_slice_in_dim(up_bias, r * ffq, ffq, 0).astype(F32)
    x = images.reshape(batch * seq, width).astype(F32)
    e = cotangent.reshape(batch * seq, width)
    e_all = gather_rep(e)
    n1, r1 = norm_rows(x)
    a1 = gather_rep((n1 * params[:, 0] + params[:, 1]).astype(BF16))
    proj = dot(a1, wq, 1, 0)
    bq = lax.dynamic_slice_in_dim(params[:, 2], r * quarter, quarter, 0)
    bv = lax.dynamic_slice_in_dim(params[:, 3], r * quarter, quarter, 0)
    group = reps * batch

    def split(t):
        return t.reshape(group, seq, heads, HEAD_DIM)

    q = split((proj[:, :quarter] + bq).astype(BF16))
    k = split(proj[:, quarter : 2 * quarter].astype(BF16))
    v = split((proj[:, 2 * quarter :] + bv).astype(BF16))
    scale = 1.0 / math.sqrt(HEAD_DIM)
    s = batched("bqhd,bkhd->bhqk", q, k) * scale
    top = jnp.max(s, axis=-1, keepdims=True)
    ex = jnp.exp(s - top)
    total = jnp.sum(ex, axis=-1, keepdims=True)
    probs = ex / total
    probs_bf = probs.astype(BF16)
    o = batched("bhqk,bkhd->bqhd", probs_bf, v).reshape(group * seq, quarter).astype(BF16)
    m = x + scatter_rep(dot(o, wo, 1, 0)) + params[:, 4]
    n2, r2 = norm_rows(m)
    a2 = gather_rep((n2 * params[:, 5] + params[:, 6]).astype(BF16))
    act, der = gelu_parts(dot(a2, wu, 1, 0) + bias_up)
    act = act.astype(BF16)
    final = m + scatter_rep(dot(act, wd, 1, 1)) + params[:, 7]
    outputs = final.astype(BF16).reshape(batch, seq, width)

    def reduce_rows(term):
        return lax.psum_scatter(term.astype(BF16), "shard", scatter_dimension=0, tiled=True)

    ef = e.astype(F32)
    g_down = reduce_rows(dot(e_all, act, 0, 0))
    du = dot(e_all, wd, 1, 0) * der
    upb = jnp.sum(du, axis=0)
    dub = du.astype(BF16)
    g_up = reduce_rows(dot(a2, dub, 0, 0))
    da2 = scatter_rep(dot(dub, wu, 1, 1))
    dm = ef + norm_back(da2 * params[:, 5], n2, r2)
    dmb = gather_rep(dm.astype(BF16))
    do = dot(dmb, wo, 1, 1).astype(BF16)
    out_term = dot(o, dmb, 0, 0).astype(BF16)
    out_term = lax.dynamic_update_slice_in_dim(
        jnp.zeros((width, width), BF16), out_term, r * quarter, 0
    )
    g_out = lax.psum_scatter(out_term, "shard", scatter_dimension=0, tiled=True)
    do = split(do)
    dv = batched("bhqk,bqhd->bkhd", probs_bf, do)
    dpr = batched("bqhd,bkhd->bhqk", do, v)
    delta = jnp.sum(probs * dpr, axis=-1, keepdims=True)
    ds = (probs * (dpr - delta) * scale).astype(BF16)
    dq = batched("bhqk,bkhd->bqhd", ds, k)
    dk = batched("bhqk,bqhd->bkhd", ds, q)
    dp = jnp.concatenate([t.reshape(group * seq, quarter) for t in (dq, dk, dv)], axis=1)
    col = jnp.sum(dp, axis=0)
    dp = dp.astype(BF16)
    g_qkv = reduce_rows(dot(a1, dp, 0, 0))
    da1 = scatter_rep(dot(dp, wq, 1, 1))
    input_grad = dm + norm_back(da1 * params[:, 0], n1, r1)
    input_grad = input_grad.astype(BF16).reshape(batch, seq, width)

    def place(piece):
        return lax.dynamic_update_slice_in_dim(jnp.zeros((width,), F32), piece, r * quarter, 0)

    vec = jnp.stack(
        [
            jnp.sum(da1 * n1, axis=0),
            jnp.sum(da1, axis=0),
            place(col[:quarter]),
            place(col[2 * quarter :]),
            jnp.sum(dm, axis=0),
            jnp.sum(da2 * n2, axis=0),
            jnp.sum(da2, axis=0),
            jnp.sum(ef, axis=0),
        ],
        axis=1,
    )
    vec = lax.psum(lax.psum_scatter(vec, "shard", scatter_dimension=0, tiled=True), "rep")
    upb = lax.all_gather(lax.psum(upb, "shard"), "rep", axis=0, tiled=True)

    def columns(g):
        return lax.all_gather(g, "rep", axis=0).transpose(1, 0, 2).astype(F32)

    g_down = columns(g_down).reshape(rows, -1)
    g_up = columns(g_up).reshape(rows, -1)
    g_qkv = columns(g_qkv).reshape(rows, reps, 3, quarter).transpose(0, 2, 1, 3).reshape(rows, -1)
    g_out = lax.psum(g_out, "rep").astype(F32)
    return (outputs, input_grad, g_qkv, g_out, g_up, g_down, vec, upb)


def solution(mesh):
    reps = mesh.shape["rep"]
    token = P(("rep", "shard"), None, None)
    row = P("shard", None)

    def body(*args):
        return per_device(reps, *args)

    return jax.shard_map(
        body,
        mesh=mesh,
        in_specs=(token, token, row, row, row, row, row, P()),
        out_specs=(token, token, row, row, row, row, row, P()),
        check_vma=False,
    )
```

profile of v0, /device:TPU:0, one launch (start us, length us, event | category | flops | bytes accessed | tf_op | source)
XLA Modules:
  0.0 929.8 jit_solution(6168868636376953412)
XLA Ops:
  9.5 32.7 %all-gather.4 = bf16[8,144,8]{1,2,0:T(8,128)(2,1)S(1)} all-gather(bf16[1,144,8]{1,2,0:T(8,128)(2,1)} %bitcast.161), channel_id=1, replica_groups=mesh['rep'=4,'shard'=8] {'shard'}, dimensions={0}, use_global_device_ids=true | all-gather | bytes 20736 | tf_op jit(solution)/shard_map/all_gather | solution.py:72
  46.0 16.3 %all-gather.18.cloned.1.call-done = bf16[1152,864]{1,0:T(8,128)(2,1)} async-done(((bf16[144,864]{1,0:T(8,128)(2,1)}), bf16[1152,864]{1,0:T(8,128)(2,1)}) %all-gather.18.cloned.1.call-update) | async-done | bytes 1990672 | tf_op jit(solution)/shard_map/all_gather | solution.py:68
  62.3 24.8 %all-gather.16.cloned.1.call-done = bf16[1024,1152]{1,0:T(8,128)(2,1)} async-done(((bf16[256,1152]{1,0:T(8,128)(2,1)}), bf16[1024,1152]{1,0:T(8,128)(2,1)}) %all-gather.16.cloned.1.call-update) | async-done | bytes 2359312 | tf_op jit(solution)/shard_map/all_gather | solution.py:45
  87.1 4.8 fusion.99
  98.7 3.2 fusion.97
  104.5 39.8 %all-gather.20.cloned.1.call-done = bf16[1152,1152]{1,0:T(8,128)(2,1)} async-done(((bf16[144,1152]{1,0:T(8,128)(2,1)}), bf16[1152,1152]{1,0:T(8,128)(2,1)}) %all-gather.20.cloned.1.call-update) | async-done | bytes 2654224 | tf_op jit(solution)/shard_map/all_gather | solution.py:69
  144.3 4.0 convolution_convert_fusion.3
  149.4 30.5 %reduce-scatter.14.cloned.1.call-done = bf16[256,1152]{1,0:T(8,128)(2,1)} async-done(((bf16[1024,1152]{1,0:T(8,128)(2,1)}), bf16[256,1152]{1,0:T(8,128)(2,1)}) %reduce-scatter.14.cloned.1.call-update) | async-done | bytes 589840 | tf_op jit(solution)/shard_map/reduce_scatter | solution.py:49
  187.7 49.8 %all-gather.24.cloned.1.call-done = bf16[1152,1076]{1,0:T(8,128)(2,1)} async-done(((bf16[144,1076]{1,0:T(8,128)(2,1)}), bf16[1152,1076]{1,0:T(8,128)(2,1)}) %all-gather.24.cloned.1.call-update) | async-done | bytes 2479120 | tf_op jit(solution)/shard_map/all_gather | solution.py:70
  237.5 24.6 %all-gather.22.cloned.1.call-done = bf16[1024,1152]{1,0:T(8,128)(2,1)} async-done(((bf16[256,1152]{1,0:T(8,128)(2,1)}), bf16[1024,1152]{1,0:T(8,128)(2,1)}) %all-gather.22.cloned.1.call-update) | async-done | bytes 2359312 | tf_op jit(solution)/shard_map/all_gather | solution.py:45
  262.1 7.5 convolution_add_fusion
  269.7 18.1 %all-gather.30.cloned.1.call-done = bf16[1,1024,1152]{2,1,0:T(8,128)(2,1)} async-done(((bf16[1,256,1152]{2,1,0:T(8,128)(2,1)}), bf16[1,1024,1152]{2,1,0:T(8,128)(2,1)}) %all-gather.30.cloned.1.call-update) | async-done | bytes 2359312 | tf_op jit(solution)/shard_map/all_gather | solution.py:45
  287.7 57.8 %all-gather.26.cloned.1.call-done = bf16[1152,1076]{1,0:T(8,128)(2,1)} async-done(((bf16[144,1076]{1,0:T(8,128)(2,1)}), bf16[1152,1076]{1,0:T(8,128)(2,1)}) %all-gather.26.cloned.1.call-update) | async-done | bytes 2479120 | tf_op jit(solution)/shard_map/all_gather | solution.py:71
  345.5 8.8 fusion.98
  355.7 5.0 convolution_convert_fusion.4
  361.1 8.8 convolution_convert_fusion.5
  370.0 7.2 convolution_convert_fusion.1
  377.3 8.3 fusion.2
  385.7 5.2 copy.96
  394.0 33.4 %reduce-scatter.16.cloned.1.call-done = bf16[256,1152]{1,0:T(8,128)(2,1)} async-done(((bf16[1024,1152]{1,0:T(8,128)(2,1)}), bf16[256,1152]{1,0:T(8,128)(2,1)}) %reduce-scatter.16.cloned.1.call-update) | async-done | bytes 589840 | tf_op jit(solution)/shard_map/reduce_scatter | solution.py:49
  427.4 2.8 fusion.93
  431.2 71.1 %reduce-scatter.26.cloned.1.call-done = bf16[144,1076]{1,0:T(8,128)(2,1)} async-done(((bf16[1152,1076]{1,0:T(8,128)(2,1)}), bf16[144,1076]{1,0:T(8,128)(2,1)}) %reduce-scatter.26.cloned.1.call-update) | async-done | bytes 309904 | tf_op jit(solution)/shard_map/reduce_scatter | solution.py:108
  502.4 74.0 %reduce-scatter.28.cloned.1.call-done = bf16[144,1076]{1,0:T(8,128)(2,1)} async-done(((bf16[1152,1076]{1,0:T(8,128)(2,1)}), bf16[144,1076]{1,0:T(8,128)(2,1)}) %reduce-scatter.28.cloned.1.call-update) | async-done | bytes 309904 | tf_op jit(solution)/shard_map/reduce_scatter | solution.py:108
  576.6 25.0 %all-gather.28.cloned.1.call-done = bf16[1024,1152]{1,0:T(8,128)(2,1)} async-done(((bf16[256,1152]{1,0:T(8,128)(2,1)}), bf16[1024,1152]{1,0:T(8,128)(2,1)}) %all-gather.28.cloned.1.call-update) | async-done | bytes 2359312 | tf_op jit(solution)/shard_map/all_gather | solution.py:45
  601.6 3.6 convolution_convert_fusion.8
  606.9 3.2 convolution_bitcast_fusion
  612.2 2.7 fusion.74
  614.9 8.4 fusion.42
  626.6 8.7 fusion.39
  640.9 4.0 convolution_convert_fusion.6
  645.2 7.0 convolution_convert_fusion.2
  658.7 21.7 %psum.23 = f32[1076]{0:T(1024)S(1)} all-reduce(f32[1076]{0:T(1024)S(1)} %get-tuple-element.44), channel_id=1, replica_groups=mesh['rep'=4,'shard'=8] {'shard'}, use_global_device_ids=true, to_apply=%region_30.0 | all-reduce | flops 1076 | bytes 8608 | tf_op jit(solution)/shard_map/psum | solution.py:157
  682.3 2.6 copy.89
  684.9 3.9 reshape.152
  690.4 2.6 copy.91
  693.0 3.9 reshape.154
  696.9 2.4 reduce_sum.174
  699.8 12.9 %reduce-scatter.22.cloned.1.call-done = bf16[144,864]{1,0:T(8,128)(2,1)} async-done(((bf16[1152,864]{1,0:T(8,128)(2,1)}), bf16[144,864]{1,0:T(8,128)(2,1)}) %reduce-scatter.22.cloned.1.call-update) | async-done | bytes 248848 | tf_op jit(solution)/shard_map/reduce_scatter | solution.py:108
  712.7 10.4 %all-gather.1 = bf16[576,864]{1,0:T(8,128)(2,1)S(1)} all-gather(bf16[144,864]{1,0:T(8,128)(2,1)} %reduce-scatter.22.cloned.1.call-done), channel_id=3, replica_groups=mesh['rep'=4,'shard'=8] {'rep'}, dimensions={0}, use_global_device_ids=true | all-gather | bytes 1244160 | tf_op jit(solution)/shard_map/all_gather | solution.py:160
  724.5 5.2 reshape.159
  729.8 5.7 copy.88
  735.4 3.6 reshape.150
  739.0 7.9 reduce-scatter.20.cloned.1.call-done
  749.8 72.2 %reduce-scatter.24.cloned.1.call-done = bf16[144,1152]{1,0:T(8,128)(2,1)} async-done(((bf16[1152,1152]{1,0:T(8,128)(2,1)}), bf16[144,1152]{1,0:T(8,128)(2,1)}) %reduce-scatter.24.cloned.1.call-update) | async-done | bytes 331792 | tf_op jit(solution)/shard_map/reduce_scatter | solution.py:124
  822.1 2.4 fusion.70
  824.5 63.2 %reduce-scatter.30.cloned.1.call-done = f32[144,8]{1,0:T(8,128)} async-done(((f32[1152,8]{1,0:T(8,128)}), f32[144,8]{1,0:T(8,128)}) %reduce-scatter.30.cloned.1.call-update) | async-done | bytes 4624
  888.6 10.9 %all-reduce.1 = (f32[144,8]{0,1:T(8,128)}, f32[4304]{0:T(1024)}) all-reduce(f32[144,8]{0,1:T(8,128)S(1)} %copy.99, f32[4304]{0:T(1024)S(1)} %dynamic-update-slice), channel_id=1, replica_groups=mesh['rep'=4,'shard'=8] {'rep'}, use_global_device_ids=true, to_apply=%region_28.0 | all-reduce | flops 5456 | bytes 43648 | tf_op jit(solution)/shard_map/psum | solution.py:156
  899.5 21.2 %all-reduce.4.cloned.1.call-done = bf16[144,1152]{1,0:T(8,128)(2,1)} async-done(((bf16[144,1152]{1,0:T(8,128)(2,1)}), bf16[144,1152]{1,0:T(8,128)(2,1)}) %all-reduce.4.cloned.1.call-update) | async-done | bytes 331792 | tf_op jit(solution)/shard_map/psum | solution.py:165
  (160 shorter events, 59.9 us)
Async XLA Ops:
  7.2 141.2 %copy-start = (bf16[144,4304]{1,0:T(8,128)(2,1)S(1)}, bf16[144,4304]{1,0:T(8,128)(2,1)}, u32[]{:S(2)}) copy-start(bf16[144,4304]{1,0:T(8,128)(2,1)} %param.12) | copy-start | bytes 3718660
  7.2 36.4 %copy-start.2 = (bf16[1,256,1152]{2,1,0:T(8,128)(2,1)S(1)}, bf16[1,256,1152]{2,1,0:T(8,128)(2,1)}, u32[]{:S(2)}) copy-start(bf16[1,256,1152]{2,1,0:T(8,128)(2,1)} %param.8) | copy-start | bytes 1769476
  7.2 55.1 %all-gather.18.cloned.1.call-start = ((), (), s32[]{:S(2)}) async-start(), calls=%async_computation.10 | async-start | bytes 2322432 | tf_op jit(solution)/shard_map/all_gather | solution.py:68
  9.5 77.6 %all-gather.16.cloned.1.call-start = ((), (), s32[]{:S(2)}) async-start(), calls=%async_computation.9 | async-start | bytes 2949120 | tf_op jit(solution)/shard_map/all_gather | solution.py:45
  45.1 99.2 %all-gather.20.cloned.1.call-start = ((), (), s32[]{:S(2)}) async-start(), calls=%async_computation.11 | async-start | bytes 2985984 | tf_op jit(solution)/shard_map/all_gather | solution.py:69
  45.8 134.0 %reduce-scatter.14.cloned.1.call-start = ((), (), s32[]{:S(2)}) async-start(), calls=%async_computation.12 | async-start | bytes 2949120 | tf_op jit(solution)/shard_map/reduce_scatter | solution.py:49
  94.7 4.0 copy-start.9
  96.7 5.3 copy-start.12
  102.0 2.0 copy-start.8
  104.5 43.8 %copy-start.16 = (bf16[36,8,4,256]{3,1,2,0:T(8,128)(2,1)}, bf16[36,8,4,256]{3,1,2,0:T(8,128)(2,1)S(1)}, u32[]{:S(2)}) copy-start(bf16[36,8,4,256]{3,1,2,0:T(8,128)(2,1)S(1)} %copy.100) | copy-start | bytes 1769476
  148.3 89.1 %all-gather.24.cloned.1.call-start = ((), (), s32[]{:S(2)}) async-start(), calls=%async_computation.14 | async-start | bytes 2985984 | tf_op jit(solution)/shard_map/all_gather | solution.py:70
  149.3 112.8 %all-gather.22.cloned.1.call-start = ((), (), s32[]{:S(2)}) async-start(), calls=%async_computation.13 | async-start | bytes 2949120 | tf_op jit(solution)/shard_map/all_gather | solution.py:45
  179.9 2.9 copy-start.3
  183.9 103.8 %all-gather.30.cloned.1.call-start = ((), (), s32[]{:S(2)}) async-start(), calls=%async_computation.24 | async-start | bytes 2949120 | tf_op jit(solution)/shard_map/all_gather | solution.py:45
  184.7 160.8 %all-gather.26.cloned.1.call-start = ((), (), s32[]{:S(2)}) async-start(), calls=%async_computation.15 | async-start | bytes 2985984 | tf_op jit(solution)/shard_map/all_gather | solution.py:71
  186.7 205.5 %reduce-scatter.18.cloned.1.call-start = ((), (), s32[]{:S(2)}) async-start(), calls=%async_computation.17 | async-start | bytes 2949120 | tf_op jit(solution)/shard_map/reduce_scatter | solution.py:49
  345.5 10.2 %copy-start.18 = (bf16[1152,1076]{1,0:T(8,128)(2,1)S(1)}, bf16[1152,1076]{1,0:T(8,128)(2,1)}, u32[]{:S(2)}) copy-start(bf16[1152,1076]{1,0:T(8,128)(2,1)} %all-gather.24.cloned.1.call-done) | copy-start | bytes 7437316
  354.3 1.4 copy-start.22
  360.7 66.7 %reduce-scatter.16.cloned.1.call-start = ((), (), s32[]{:S(2)}) async-start(), calls=%async_computation.16 | async-start | bytes 2949120 | tf_op jit(solution)/shard_map/reduce_scatter | solution.py:49
  370.0 132.3 %reduce-scatter.26.cloned.1.call-start = ((), (), s32[]{:S(2)}) async-start(), calls=%async_computation.23 | async-start | bytes 2985984 | tf_op jit(solution)/shard_map/reduce_scatter | solution.py:108
  377.3 199.1 %reduce-scatter.28.cloned.1.call-start = ((), (), s32[]{:S(2)}) async-start(), calls=%async_computation.27 | async-start | bytes 2985984 | tf_op jit(solution)/shard_map/reduce_scatter | solution.py:108
  390.9 36.5 %copy-start.5 = (bf16[1,256,1152]{2,1,0:T(8,128)(2,1)S(1)}, bf16[1,256,1152]{2,1,0:T(8,128)(2,1)}, u32[]{:S(2)}) copy-start(bf16[1,256,1152]{2,1,0:T(8,128)(2,1)} %param.9) | copy-start | bytes 1769476
  390.9 210.6 %all-gather.28.cloned.1.call-start = ((), (), s32[]{:S(2)}) async-start(), calls=%async_computation.18 | async-start | bytes 2949120 | tf_op jit(solution)/shard_map/all_gather | solution.py:45
  431.2 249.7 %all-gather.32.cloned.1.call-start = ((), (), s32[]{:S(2)}) async-start(), calls=%async_computation.25 | async-start | bytes 1658880 | tf_op jit(solution)/shard_map/all_gather | solution.py:160
  502.3 186.5 %all-gather.34.cloned.1.call-start = ((), (), s32[]{:S(2)}) async-start(), calls=%async_computation.26 | async-start | bytes 1658880 | tf_op jit(solution)/shard_map/all_gather | solution.py:160
  576.4 136.3 %reduce-scatter.22.cloned.1.call-start = ((), (), s32[]{:S(2)}) async-start(), calls=%async_computation.20 | async-start | bytes 2322432 | tf_op jit(solution)/shard_map/reduce_scatter | solution.py:108
  606.9 3.2 copy-start.14
  610.1 2.0 copy-start.13
  610.9 1.3 copy-start.15
  612.2 2.7 copy-start.11
  623.2 3.3 copy-start.10
  637.3 1.3 copy-start.7
  637.6 1.4 copy-start.6
  638.6 2.3 copy-start.19
  639.1 1.8 copy-start.4
  644.9 102.0 %reduce-scatter.20.cloned.1.call-start = ((), (), s32[]{:S(2)}) async-start(), calls=%async_computation.19 | async-start | bytes 2949120 | tf_op jit(solution)/shard_map/reduce_scatter | solution.py:49
  652.2 1.8 copy-start.17
  652.2 169.8 %reduce-scatter.24.cloned.1.call-start = ((), (), s32[]{:S(2)}) async-start(), calls=%async_computation.21 | async-start | bytes 2985984 | tf_op jit(solution)/shard_map/reduce_scatter | solution.py:124
  652.3 2.8 copy-start.20
  656.8 0.7 copy-start.21
  656.9 230.8 %reduce-scatter.30.cloned.1.call-start = ((), (), s32[]{:S(2)}) async-start(), calls=%async_computation.28 | async-start | bytes 663552
  749.7 172.8 %copy-start.1 = (bf16[144,4304]{1,0:T(8,128)(2,1)S(1)}, bf16[144,4304]{1,0:T(8,128)(2,1)}, u32[]{:S(2)}) copy-start(bf16[144,4304]{1,0:T(8,128)(2,1)} %param.12) | copy-start | bytes 3718660
  749.8 170.9 %all-reduce.4.cloned.1.call-start = ((), (), s32[]{:S(2)}) async-start(), calls=%async_computation.22 | async-start | bytes 663552 | tf_op jit(solution)/shard_map/psum | solution.py:165
Sparse Core Ops, SparseCore 0:
  10.8 51.4 all-gather.17
  64.4 22.6 all-gather.15
  89.3 54.9 all-gather.19
  148.4 31.3 reduce-scatter.13
  182.5 54.9 all-gather.23
  239.5 22.6 all-gather.21
  263.7 24.0 all-gather.29
  290.5 54.9 all-gather.25
  360.8 31.3 reduce-scatter.17
  394.6 32.8 reduce-scatter.15
  431.1 71.1 reduce-scatter.25
  505.8 70.4 reduce-scatter.27
  578.5 23.0 all-gather.27
  603.0 18.2 all-gather.31
  622.7 18.2 all-gather.33
  645.0 67.6 reduce-scatter.21
  715.1 31.7 reduce-scatter.19
  750.4 71.6 reduce-scatter.23
  825.9 61.6 reduce-scatter.29
  889.9 30.7 all-reduce.3
where the time goes:
time: 939 us; the launch traced here: 930 us
  waiting for transfers between devices  645 us (69%)
  matrix products  96.5 us (10%)
  blocking collectives  75.6 us (8%)
  local copies, waits for them, and re-layouts  63.5 us (7%)
  other arithmetic  30.9 us (3%)
  between operations  15.9 us (2%)
    reduce_scatter x3, waiting for transfers between devices, reduce_rows(): lax.psum_scatter(term.astype(BF16), 'shard', scatter_dimension=0, tiled=T...  158 us
    all_gather x4, waiting for transfers between devices, gather_rep(): return lax.all_gather(a, 'rep', axis=0, tiled=True)  92.5 us
    reduce_scatter x4, waiting for transfers between devices, scatter_rep(): lax.psum_scatter(a.astype(BF16), 'rep', scatter_dimension=0, tiled=True)  73.1 us
    reduce_scatter x1, waiting for transfers between devices, per_device(): g_out = lax.psum_scatter(out_term, 'shard', scatter_dimension=0, tiled=True)  72.2 us
    dot_general x12, matrix products, dot(): lax.dot_general(a, b, (((ca,), (cb,)), ((), ())), preferred_element_type=...  71 us
    unnamed x21, waiting for transfers between devices  64.9 us
    all_gather x1, waiting for transfers between devices, per_device(): wd = lax.all_gather(mine_down, 'shard', axis=0, tiled=True)  57.8 us
    all_gather x1, waiting for transfers between devices, per_device(): wu = lax.all_gather(mine_up, 'shard', axis=0, tiled=True)  49.8 us
  transfers between devices with their start and end apart: 20, of which 18 were waited for; matrix products, arithmetic and copies ran while one was open for 17% of the time, Pallas kernels for 0%

commit v1 on v0

--- a/solution.py
+++ b/solution.py
@@ -1,3 +1,4 @@
+import functools
 import math
 import jax
 import jax.numpy as jnp
@@ -12,6 +13,27 @@
 BF16 = jnp.bfloat16
 
 
+def units_build(unit, axis_key):
+    n_chips = lax.axis_size(axis_key)
+    met_up = range(n_chips)
+    v_next = map(lambda no: (no, (no + 1) % n_chips), met_up)
+    line_up = list(v_next)
+    mixed_arr = range(n_chips)
+    front = map(lambda no: (no, (no - 1) % n_chips), mixed_arr)
+    u_next, later = ([unit], [unit])
+    row_list = list(front)
+    for _ in range(n_chips // 2):
+        u_next.append(lax.ppermute(u_next[-1], axis_name=axis_key, perm=line_up))
+    for _ in [*range((n_chips - 1) // 2)]:
+        part_next = lax.ppermute(later[-1], axis_name=axis_key, perm=row_list)
+        later.append(part_next)
+    t_next = jnp.concatenate([*u_next[::-1], *later[1:]], 0)
+    return jnp.roll(t_next, (lax.axis_index(axis_key) - n_chips // 2) * unit.shape[0], 0)
+
+
+_unite_zones = functools.partial(units_build, axis_key="rep")
+
+
 def dot(a, b, ca, cb):
     return lax.dot_general(a, b, (((ca,), (cb,)), ((), ())), preferred_element_type=F32)
 
@@ -42,7 +64,7 @@
 
 
 def gather_rep(a):
-    return lax.all_gather(a, "rep", axis=0, tiled=True)
+    return _unite_zones(a)
 
 
 def scatter_rep(a):

time: 939 us -> 846 us (0.901)
  waiting for transfers between devices: 645 us -> 514 us
  other arithmetic: 30.9 us -> 70.8 us
    all_gather x4 -> x0, waiting for transfers between devices: 92.5 us -> none  [gather_rep(): return lax.all_gather(a, 'rep', axis=0, tiled=True)]
    ppermute x0 -> x12, waiting for transfers between devices: none -> 58 us  [the longest x8 56.9 us: units_build(): u_next.append(lax.ppermute(u_next[-1], axis_name=axis_key, perm=line_up))]
    all_gather x1, waiting for transfers between devices: 49.8 us -> 3.71 us  [per_device(): wu = lax.all_gather(mine_up, 'shard', axis=0, tiled=True)]
    concatenate x0 -> x4, other arithmetic: none -> 42.5 us  [units_build(): jnp.roll(t_next, (lax.axis_index(axis_key) - n_chips // 2) * unit.shape[0...]
    all_gather x1, waiting for transfers between devices: 39.8 us -> 22.1 us  [per_device(): wo = lax.all_gather(w_out, 'shard', axis=0, tiled=True)]
    all_gather x1, waiting for transfers between devices: 16.3 us -> 0.01 us  [per_device(): wq = lax.all_gather(part, 'shard', axis=0, tiled=True)]
    reduce_scatter x3, waiting for transfers between devices: 158 us -> 146 us  [reduce_rows(): lax.psum_scatter(term.astype(BF16), 'shard', scatter_dimension=0, tiled=T...]
    unnamed x21 -> x17, waiting for transfers between devices: 64.9 us -> 64.1 us
  transfers between devices with their start and end apart: 20 -> 28, of which waited for: 18 -> 20; matrix products, arithmetic and copies ran while one was open for 17% -> 23% of each run, Pallas kernels for 0% -> 0%
where the time goes in v1:
time: 846 us; the launch traced here: 835 us
  waiting for transfers between devices  514 us (61%)
  matrix products  94.7 us (11%)
  blocking collectives  73.4 us (9%)
  other arithmetic  70.8 us (8%)
  local copies, waits for them, and re-layouts  58 us (7%)
  between operations  15.6 us (2%)
  starting transfers between devices  8.82 us (1%)
    reduce_scatter x3, waiting for transfers between devices, reduce_rows(): lax.psum_scatter(term.astype(BF16), 'shard', scatter_dimension=0, tiled=T...  146 us
    reduce_scatter x4, waiting for transfers between devices, scatter_rep(): lax.psum_scatter(a.astype(BF16), 'rep', scatter_dimension=0, tiled=True)  77.9 us
    reduce_scatter x1, waiting for transfers between devices, per_device(): g_out = lax.psum_scatter(out_term, 'shard', scatter_dimension=0, tiled=True)  72.3 us
    dot_general x12, matrix products, dot(): lax.dot_general(a, b, (((ca,), (cb,)), ((), ())), preferred_element_type=...  69.2 us
    unnamed x17, waiting for transfers between devices  64.1 us
    ppermute x8, waiting for transfers between devices, units_build(): u_next.append(lax.ppermute(u_next[-1], axis_name=axis_key, perm=line_up))  56.9 us
    all_gather x1, waiting for transfers between devices, per_device(): wd = lax.all_gather(mine_down, 'shard', axis=0, tiled=True)  48.6 us
    concatenate x4, other arithmetic, units_build(): jnp.roll(t_next, (lax.axis_index(axis_key) - n_chips // 2) * unit.shape[0...  42.5 us
  transfers between devices with their start and end apart: 28, of which 20 were waited for; matrix products, arithmetic and copies ran while one was open for 23% of the time, Pallas kernels for 0%

profile of v1, /device:TPU:0, one launch (start us, length us, event | category | flops | bytes accessed | tf_op | source)
XLA Modules:
  0.0 834.8 jit_solution(12555434138884190740)
XLA Ops:
  10.3 32.7 %all-gather.3 = bf16[8,144,8]{1,2,0:T(8,128)(2,1)S(1)} all-gather(bf16[1,144,8]{1,2,0:T(8,128)(2,1)} %bitcast.153), channel_id=1, replica_groups=mesh['rep'=4,'shard'=8] {'shard'}, dimensions={0}, use_global_device_ids=true | all-gather | bytes 20736 | tf_op jit(solution)/shard_map/all_gather | solution.py:94
  46.9 12.1 %collective-permute-done = bf16[256,1152]{1,0:T(8,128)(2,1)S(1)} collective-permute-done((bf16[256,1152]{1,0:T(8,128)(2,1)S(1)}, bf16[256,1152]{1,0:T(8,128)(2,1)S(1)}, u32[]{:S(2)}, u32[]{:S(2)}) %collective-permute-start) | collective-permute-done | bytes 589856 | tf_op jit(solution)/shard_map/ppermute | solution.py:26
  59.7 8.6 %collective-permute-done.1 = bf16[256,1152]{1,0:T(8,128)(2,1)} collective-permute-done((bf16[256,1152]{1,0:T(8,128)(2,1)S(1)}, bf16[256,1152]{1,0:T(8,128)(2,1)}, u32[]{:S(2)}, u32[]{:S(2)}) %collective-permute-start.1) | collective-permute-done | bytes 589856 | tf_op jit(solution)/shard_map/ppermute | solution.py:26
  68.4 10.1 %fusion.44 = bf16[1024,1152]{1,0:T(8,128)(2,1)} fusion(s32[]{:T(128)S(6)} %select_n.44, bf16[256,1152]{1,0:T(8,128)(2,1)} %collective-permute-done.1, bf16[256,1152]{1,0:T(8,128)(2,1)S(1)} %collective-permute-done, bf16[256,1152]{1,0:T(8,128)(2,1)S(1)} %fusion.71, bf16[256,1152]{1,0:T(8,128)(2,1)} %collective-permute-done.2), kind=kLoop, calls=%fused_computation.87 | loop fusion | flops 18874368 | bytes 4718596 | tf_op jit(solution)/shard_map/jit(_roll_dynamic)/concatenate | solution.py:31
  78.5 4.9 fusion.121
  90.1 3.2 fusion.119
  95.9 22.1 %all-gather.13.cloned.1.call-done = bf16[1152,1152]{1,0:T(8,128)(2,1)} async-done(((bf16[144,1152]{1,0:T(8,128)(2,1)}), bf16[1152,1152]{1,0:T(8,128)(2,1)}) %all-gather.13.cloned.1.call-update) | async-done | bytes 2654224 | tf_op jit(solution)/shard_map/all_gather | solution.py:91
  118.0 4.0 convolution_convert_fusion.3
  125.5 28.1 %reduce-scatter.12.cloned.1.call-done = bf16[256,1152]{1,0:T(8,128)(2,1)} async-done(((bf16[1024,1152]{1,0:T(8,128)(2,1)}), bf16[256,1152]{1,0:T(8,128)(2,1)}) %reduce-scatter.12.cloned.1.call-update) | async-done | bytes 589840 | tf_op jit(solution)/shard_map/reduce_scatter | solution.py:71
  161.2 10.7 %collective-permute-done.3 = bf16[256,1152]{1,0:T(8,128)(2,1)S(1)} collective-permute-done((bf16[256,1152]{1,0:T(8,128)(2,1)S(1)}, bf16[256,1152]{1,0:T(8,128)(2,1)S(1)}, u32[]{:S(2)}, u32[]{:S(2)}) %collective-permute-start.3) | collective-permute-done | bytes 589856 | tf_op jit(solution)/shard_map/ppermute | solution.py:26
  172.4 12.2 %collective-permute-done.7 = bf16[256,1152]{1,0:T(8,128)(2,1)S(1)} collective-permute-done((bf16[256,1152]{1,0:T(8,128)(2,1)S(1)}, bf16[256,1152]{1,0:T(8,128)(2,1)S(1)}, u32[]{:S(2)}, u32[]{:S(2)}) %collective-permute-start.7) | collective-permute-done | bytes 589856 | tf_op jit(solution)/shard_map/ppermute | solution.py:26
  184.5 11.4 %fusion.30 = bf16[1024,1152]{1,0:T(8,128)(2,1)} fusion(s32[]{:T(128)S(6)} %select_n.44, bf16[256,1152]{1,0:T(8,128)(2,1)S(1)} %collective-permute-done.7, bf16[256,1152]{1,0:T(8,128)(2,1)S(1)} %collective-permute-done.6, bf16[256,1152]{1,0:T(8,128)(2,1)S(1)} %bitcast.147, bf16[256,1152]{1,0:T(8,128)(2,1)S(1)} %collective-permute-done.8), kind=kLoop, calls=%fused_computation.73 | loop fusion | flops 18874368 | bytes 4718596 | tf_op jit(solution)/shard_map/jit(_roll_dynamic)/concatenate | solution.py:31
  196.0 11.5 %fusion.37 = bf16[1024,1152]{1,0:T(8,128)(2,1)} fusion(s32[]{:T(128)S(6)} %select_n.44, bf16[256,1152]{1,0:T(8,128)(2,1)S(1)} %collective-permute-done.4, bf16[256,1152]{1,0:T(8,128)(2,1)S(1)} %collective-permute-done.3, bf16[256,1152]{1,0:T(8,128)(2,1)S(1)} %add_convert_fusion.1, bf16[256,1152]{1,0:T(8,128)(2,1)S(1)} %collective-permute-done.5), kind=kLoop, calls=%fused_computation.80 | loop fusion | flops 18874368 | bytes 4718596 | tf_op jit(solution)/shard_map/jit(_roll_dynamic)/concatenate | solution.py:31
  207.5 3.7 all-gather.15.cloned.1.call-done
  211.2 7.5 convolution_add_fusion
  218.8 48.6 %all-gather.17.cloned.1.call-done = bf16[1152,1076]{1,0:T(8,128)(2,1)} async-done(((bf16[144,1076]{1,0:T(8,128)(2,1)}), bf16[1152,1076]{1,0:T(8,128)(2,1)}) %all-gather.17.cloned.1.call-update) | async-done | bytes 2479120 | tf_op jit(solution)/shard_map/all_gather | solution.py:93
  267.4 9.1 %fusion.120 = (f32[1076]{0:T(1024)S(1)}, bf16[1024,1076]{0,1:T(8,128)(2,1)S(1)}) fusion(f32[1024,1076]{0,1:T(8,128)} %convolution_add_fusion, bf16[1024,1152]{1,0:T(8,128)(2,1)} %fusion.30, bf16[1152,1076]{1,0:T(8,128)(2,1)} %all-gather.17.cloned.1.call-done), kind=kOutput, calls=%fused_computation.207 | convolution fusion | flops 2560637952 | bytes 11453648 | tf_op jit(solution)/shard_map/dot_general | solution.py:38
  277.9 5.0 convolution_convert_fusion.4
  282.9 7.1 convolution_convert_fusion.1
  290.5 8.9 %convolution_convert_fusion.5 = bf16[1024,1152]{1,0:T(8,128)(2,1)} fusion(bf16[1152,1076]{1,0:T(8,128)(2,1)} %all-gather.17.cloned.1.call-done, f32[1024,1076]{0,1:T(8,128)} %convolution_add_fusion), kind=kOutput, calls=%fused_computation.53 | convolution fusion | flops 2549698560 | bytes 9245696 | tf_op jit(solution)/shard_map/dot_general | solution.py:38
  299.4 8.0 convolution_convert_fusion
  307.5 7.0 reduce-scatter.16.cloned.1.call-done
  316.2 73.7 %reduce-scatter.24.cloned.1.call-done = bf16[144,1076]{1,0:T(8,128)(2,1)} async-done(((bf16[1152,1076]{1,0:T(8,128)(2,1)}), bf16[144,1076]{1,0:T(8,128)(2,1)}) %reduce-scatter.24.cloned.1.call-update) | async-done | bytes 309904 | tf_op jit(solution)/shard_map/reduce_scatter | solution.py:130
  390.0 34.8 %reduce-scatter.14.cloned.1.call-done = bf16[256,1152]{1,0:T(8,128)(2,1)} async-done(((bf16[1024,1152]{1,0:T(8,128)(2,1)}), bf16[256,1152]{1,0:T(8,128)(2,1)}) %reduce-scatter.14.cloned.1.call-update) | async-done | bytes 589840 | tf_op jit(solution)/shard_map/reduce_scatter | solution.py:71
  424.8 2.9 fusion.116
  429.6 13.2 %collective-permute-done.9 = bf16[256,1152]{1,0:T(8,128)(2,1)S(1)} collective-permute-done((bf16[256,1152]{1,0:T(8,128)(2,1)S(1)}, bf16[256,1152]{1,0:T(8,128)(2,1)S(1)}, u32[]{:S(2)}, u32[]{:S(2)}) %collective-permute-start.9) | collective-permute-done | bytes 589856 | tf_op jit(solution)/shard_map/ppermute | solution.py:26
  442.8 57.2 %reduce-scatter.26.cloned.1.call-done = bf16[144,1076]{1,0:T(8,128)(2,1)} async-done(((bf16[1152,1076]{1,0:T(8,128)(2,1)}), bf16[144,1076]{1,0:T(8,128)(2,1)}) %reduce-scatter.26.cloned.1.call-update) | async-done | bytes 309904 | tf_op jit(solution)/shard_map/reduce_scatter | solution.py:130
  500.1 9.3 %fusion.23 = bf16[1024,1152]{1,0:T(8,128)(2,1)S(1)} fusion(s32[]{:T(128)S(6)} %select_n.44, bf16[256,1152]{1,0:T(8,128)(2,1)} %collective-permute-done.10, bf16[256,1152]{1,0:T(8,128)(2,1)S(1)} %collective-permute-done.9, bf16[256,1152]{1,0:T(8,128)(2,1)S(1)} %convert_element_type.137, bf16[256,1152]{1,0:T(8,128)(2,1)} %collective-permute-done.11), kind=kLoop, calls=%fused_computation.66 | loop fusion | flops 18874368 | bytes 4718596 | tf_op jit(solution)/shard_map/jit(_roll_dynamic)/concatenate | solution.py:31
  513.4 3.2 convolution_bitcast_fusion
  518.5 2.7 fusion.97
  521.2 8.6 %fusion.66 = f32[4,256,4,72]{1,3,2,0:T(8,128)} fusion(f32[4,4,256,256]{2,3,1,0:T(8,128)} %fusion.97, bf16[4,256,4,72]{1,0,3,2:T(4,128)(2,1)} %reshape.133, f32[4,4,256,256]{2,3,1,0:T(8,128)} %copy-done.6, f32[4,4,256]{2,1,0:T(4,128)S(1)} %get-tuple-element.44), kind=kOutput, calls=%fused_computation.119 | convolution fusion | flops 158339328 | bytes 10174464 | tf_op jit(solution)/shard_map/bhqk,bqhd->bkhd/dot_general | solution.py:42
  533.1 8.5 %fusion.63 = f32[4,256,4,72]{1,3,2,0:T(8,128)} fusion(f32[4,4,256,256]{2,3,1,0:T(8,128)} %fusion.97, bf16[4,256,4,72]{1,0,3,2:T(4,128)(2,1)} %copy-done.12, f32[4,4,256,256]{2,3,1,0:T(8,128)} %copy-done.6, f32[4,4,256]{2,1,0:T(4,128)S(1)} %get-tuple-element.44), kind=kOutput, calls=%fused_computation.118 | convolution fusion | flops 158339328 | bytes 10174464 | tf_op jit(solution)/shard_map/bhqk,bkhd->bqhd/dot_general | solution.py:42
  546.8 4.0 convolution_convert_fusion.6
  551.1 7.0 convolution_convert_fusion.2
  564.6 19.5 %psum.23 = f32[1076]{0:T(1024)S(1)} all-reduce(f32[1076]{0:T(1024)S(1)} %get-tuple-element.46), channel_id=1, replica_groups=mesh['rep'=4,'shard'=8] {'shard'}, use_global_device_ids=true, to_apply=%region_30.32 | all-reduce | flops 1076 | bytes 8608 | tf_op jit(solution)/shard_map/psum | solution.py:179
  588.7 2.5 copy.88
  591.3 3.9 reshape.152
  599.3 3.9 reshape.154
  603.2 14.6 %reduce-scatter.20.cloned.1.call-done = bf16[144,864]{1,0:T(8,128)(2,1)} async-done(((bf16[1152,864]{1,0:T(8,128)(2,1)}), bf16[144,864]{1,0:T(8,128)(2,1)}) %reduce-scatter.20.cloned.1.call-update) | async-done | bytes 248848 | tf_op jit(solution)/shard_map/reduce_scatter | solution.py:130
  617.8 10.4 %all-gather = bf16[576,864]{1,0:T(8,128)(2,1)S(1)} all-gather(bf16[144,864]{1,0:T(8,128)(2,1)} %reduce-scatter.20.cloned.1.call-done), channel_id=2, replica_groups=mesh['rep'=4,'shard'=8] {'rep'}, dimensions={0}, use_global_device_ids=true | all-gather | bytes 1244160 | tf_op jit(solution)/shard_map/all_gather | solution.py:182
  629.6 5.2 reshape.159
  634.9 5.7 copy.87
  640.5 3.6 reshape.150
  644.1 8.1 reduce-scatter.18.cloned.1.call-done
  655.1 72.3 %reduce-scatter.22.cloned.1.call-done = bf16[144,1152]{1,0:T(8,128)(2,1)} async-done(((bf16[1152,1152]{1,0:T(8,128)(2,1)}), bf16[144,1152]{1,0:T(8,128)(2,1)}) %reduce-scatter.22.cloned.1.call-update) | async-done | bytes 331792 | tf_op jit(solution)/shard_map/reduce_scatter | solution.py:146
  729.8 63.1 %reduce-scatter.28.cloned.1.call-done = f32[144,8]{1,0:T(8,128)} async-done(((f32[1152,8]{1,0:T(8,128)}), f32[144,8]{1,0:T(8,128)}) %reduce-scatter.28.cloned.1.call-update) | async-done | bytes 4624
  793.9 10.9 %all-reduce.1 = (f32[144,8]{0,1:T(8,128)}, f32[4304]{0:T(1024)}) all-reduce(f32[144,8]{0,1:T(8,128)S(1)} %copy.95, f32[4304]{0:T(1024)S(1)} %dynamic-update-slice), channel_id=1, replica_groups=mesh['rep'=4,'shard'=8] {'rep'}, use_global_device_ids=true, to_apply=%region_28.30 | all-reduce | flops 5456 | bytes 43648 | tf_op jit(solution)/shard_map/psum | solution.py:178
  804.7 21.2 %all-reduce.4.cloned.1.call-done = bf16[144,1152]{1,0:T(8,128)(2,1)} async-done(((bf16[144,1152]{1,0:T(8,128)(2,1)}), bf16[144,1152]{1,0:T(8,128)(2,1)}) %all-reduce.4.cloned.1.call-update) | async-done | bytes 331792 | tf_op jit(solution)/shard_map/psum | solution.py:187
  (172 shorter events, 72.5 us)
Async XLA Ops:
  7.2 115.3 %copy-start = (bf16[144,4304]{1,0:T(8,128)(2,1)S(1)}, bf16[144,4304]{1,0:T(8,128)(2,1)}, u32[]{:S(2)}) copy-start(bf16[144,4304]{1,0:T(8,128)(2,1)} %param.14) | copy-start | bytes 3718660
  7.2 37.2 %copy-start.2 = (bf16[1,256,1152]{2,1,0:T(8,128)(2,1)S(1)}, bf16[1,256,1152]{2,1,0:T(8,128)(2,1)}, u32[]{:S(2)}) copy-start(bf16[1,256,1152]{2,1,0:T(8,128)(2,1)} %param.10) | copy-start | bytes 1769476
  7.2 71.3 %all-gather.11.cloned.1.call-start = ((), (), s32[]{:S(2)}) async-start(), calls=%async_computation.9 | async-start | bytes 2322432 | tf_op jit(solution)/shard_map/all_gather | solution.py:90
  9.5 108.5 %all-gather.13.cloned.1.call-start = ((), (), s32[]{:S(2)}) async-start(), calls=%async_computation.10 | async-start | bytes 2985984 | tf_op jit(solution)/shard_map/all_gather | solution.py:91
  10.2 143.4 %reduce-scatter.12.cloned.1.call-start = ((), (), s32[]{:S(2)}) async-start(), calls=%async_computation.11 | async-start | bytes 2949120 | tf_op jit(solution)/shard_map/reduce_scatter | solution.py:71
  45.1 13.9 %collective-permute-start = (bf16[256,1152]{1,0:T(8,128)(2,1)S(1)}, bf16[256,1152]{1,0:T(8,128)(2,1)S(1)}, u32[]{:S(2)}, u32[]{:S(2)}) collective-permute-start(bf16[256,1152]{1,0:T(8,128)(2,1)S(1)} %fusion.71), channel_id=1, source_target_pairs={{0,8},{8,16},{16,24},{24,0},{1,9},{9,17},{17,25},{25,1},{2,10},{10... | collective-permute-start | bytes 1769480 | tf_op jit(solution)/shard_map/ppermute | solution.py:26
  45.1 14.6 %collective-permute-start.2 = (bf16[256,1152]{1,0:T(8,128)(2,1)S(1)}, bf16[256,1152]{1,0:T(8,128)(2,1)}, u32[]{:S(2)}, u32[]{:S(2)}) collective-permute-start(bf16[256,1152]{1,0:T(8,128)(2,1)S(1)} %fusion.71), channel_id=1, source_target_pairs={{0,24},{8,0},{16,8},{24,16},{1,25},{9,1},{17,9},{25,17},{2,26},{10... | collective-permute-start | bytes 1769480 | tf_op jit(solution)/shard_map/ppermute | solution.py:28
  59.0 9.4 %collective-permute-start.1 = (bf16[256,1152]{1,0:T(8,128)(2,1)S(1)}, bf16[256,1152]{1,0:T(8,128)(2,1)}, u32[]{:S(2)}, u32[]{:S(2)}) collective-permute-start(bf16[256,1152]{1,0:T(8,128)(2,1)S(1)} %collective-permute-done), channel_id=1, source_target_pairs={{0,8},{8,16},{16,24},{24,0},{1,9},{9,17},{17,25},{25,1},{2,10},{10... | collective-permute-start | bytes 1769480 | tf_op jit(solution)/shard_map/ppermute | solution.py:26
  86.1 4.0 copy-start.12
  88.1 5.3 copy-start.13
  93.4 2.0 copy-start.6
  95.9 22.1 %copy-start.17 = (bf16[36,8,4,256]{3,1,2,0:T(8,128)(2,1)}, bf16[36,8,4,256]{3,1,2,0:T(8,128)(2,1)S(1)}, u32[]{:S(2)}) copy-start(bf16[36,8,4,256]{3,1,2,0:T(8,128)(2,1)S(1)} %copy.96) | copy-start | bytes 1769476
  122.0 1.4 copy-start.7
  122.1 89.2 %all-gather.15.cloned.1.call-start = ((), (), s32[]{:S(2)}) async-start(), calls=%async_computation.12 | async-start | bytes 2985984 | tf_op jit(solution)/shard_map/all_gather | solution.py:92
  123.4 144.0 %all-gather.17.cloned.1.call-start = ((), (), s32[]{:S(2)}) async-start(), calls=%async_computation.13 | async-start | bytes 2985984 | tf_op jit(solution)/shard_map/all_gather | solution.py:93
  123.4 35.2 %collective-permute-start.6 = (bf16[256,1152]{1,0:T(8,128)(2,1)S(1)}, bf16[256,1152]{1,0:T(8,128)(2,1)S(1)}, u32[]{:S(2)}, u32[]{:S(2)}) collective-permute-start(bf16[256,1152]{1,0:T(8,128)(2,1)S(1)} %bitcast.145), channel_id=1, source_target_pairs={{0,8},{8,16},{16,24},{24,0},{1,9},{9,17},{17,25},{25,1},{2,10},{10... | collective-permute-start | bytes 1769480 | tf_op jit(solution)/shard_map/ppermute | solution.py:26
  125.4 189.0 %reduce-scatter.16.cloned.1.call-start = ((), (), s32[]{:S(2)}) async-start(), calls=%async_computation.15 | async-start | bytes 2949120 | tf_op jit(solution)/shard_map/reduce_scatter | solution.py:71
  153.6 2.9 copy-start.3
  156.8 15.0 %collective-permute-start.3 = (bf16[256,1152]{1,0:T(8,128)(2,1)S(1)}, bf16[256,1152]{1,0:T(8,128)(2,1)S(1)}, u32[]{:S(2)}, u32[]{:S(2)}) collective-permute-start(bf16[256,1152]{1,0:T(8,128)(2,1)S(1)} %add_convert_fusion.1), channel_id=1, source_target_pairs={{0,8},{8,16},{16,24},{24,0},{1,9},{9,17},{17,25},{25,1},{2,10},{10... | collective-permute-start | bytes 1769480 | tf_op jit(solution)/shard_map/ppermute | solution.py:26
  156.9 15.5 %collective-permute-start.8 = (bf16[256,1152]{1,0:T(8,128)(2,1)S(1)}, bf16[256,1152]{1,0:T(8,128)(2,1)S(1)}, u32[]{:S(2)}, u32[]{:S(2)}) collective-permute-start(bf16[256,1152]{1,0:T(8,128)(2,1)S(1)} %bitcast.146), channel_id=1, source_target_pairs={{0,24},{8,0},{16,8},{24,16},{1,25},{9,1},{17,9},{25,17},{2,26},{10... | collective-permute-start | bytes 1769480 | tf_op jit(solution)/shard_map/ppermute | solution.py:28
  158.6 25.9 %collective-permute-start.7 = (bf16[256,1152]{1,0:T(8,128)(2,1)S(1)}, bf16[256,1152]{1,0:T(8,128)(2,1)S(1)}, u32[]{:S(2)}, u32[]{:S(2)}) collective-permute-start(bf16[256,1152]{1,0:T(8,128)(2,1)S(1)} %collective-permute-done.6), channel_id=1, source_target_pairs={{0,8},{8,16},{16,24},{24,0},{1,9},{9,17},{17,25},{25,1},{2,10},{10... | collective-permute-start | bytes 1769480 | tf_op jit(solution)/shard_map/ppermute | solution.py:26
  159.4 36.5 %collective-permute-start.5 = (bf16[256,1152]{1,0:T(8,128)(2,1)S(1)}, bf16[256,1152]{1,0:T(8,128)(2,1)S(1)}, u32[]{:S(2)}, u32[]{:S(2)}) collective-permute-start(bf16[256,1152]{1,0:T(8,128)(2,1)S(1)} %add_convert_fusion.1), channel_id=1, source_target_pairs={{0,24},{8,0},{16,8},{24,16},{1,25},{9,1},{17,9},{25,17},{2,26},{10... | collective-permute-start | bytes 1769480 | tf_op jit(solution)/shard_map/ppermute | solution.py:28
  171.9 24.1 %collective-permute-start.4 = (bf16[256,1152]{1,0:T(8,128)(2,1)S(1)}, bf16[256,1152]{1,0:T(8,128)(2,1)S(1)}, u32[]{:S(2)}, u32[]{:S(2)}) collective-permute-start(bf16[256,1152]{1,0:T(8,128)(2,1)S(1)} %collective-permute-done.3), channel_id=1, source_target_pairs={{0,8},{8,16},{16,24},{24,0},{1,9},{9,17},{17,25},{25,1},{2,10},{10... | collective-permute-start | bytes 1769480 | tf_op jit(solution)/shard_map/ppermute | solution.py:26
  267.4 10.5 %copy-start.19 = (bf16[1152,1076]{1,0:T(8,128)(2,1)S(1)}, bf16[1152,1076]{1,0:T(8,128)(2,1)}, u32[]{:S(2)}) copy-start(bf16[1152,1076]{1,0:T(8,128)(2,1)} %all-gather.15.cloned.1.call-done) | copy-start | bytes 7437316
  276.5 1.4 copy-start.21
  282.9 107.0 %reduce-scatter.24.cloned.1.call-start = ((), (), s32[]{:S(2)}) async-start(), calls=%async_computation.20 | async-start | bytes 2985984 | tf_op jit(solution)/shard_map/reduce_scatter | solution.py:130
  290.0 134.8 %reduce-scatter.14.cloned.1.call-start = ((), (), s32[]{:S(2)}) async-start(), calls=%async_computation.14 | async-start | bytes 2949120 | tf_op jit(solution)/shard_map/reduce_scatter | solution.py:71
  299.4 200.7 %reduce-scatter.26.cloned.1.call-start = ((), (), s32[]{:S(2)}) async-start(), calls=%async_computation.21 | async-start | bytes 2985984 | tf_op jit(solution)/shard_map/reduce_scatter | solution.py:130
  307.4 117.4 %copy-start.8 = (bf16[1,256,1152]{2,1,0:T(8,128)(2,1)S(1)}, bf16[1,256,1152]{2,1,0:T(8,128)(2,1)}, u32[]{:S(2)}) copy-start(bf16[1,256,1152]{2,1,0:T(8,128)(2,1)} %param.11) | copy-start | bytes 1769476
  307.4 279.8 %all-gather.19.cloned.1.call-start = ((), (), s32[]{:S(2)}) async-start(), calls=%async_computation.22 | async-start | bytes 1658880 | tf_op jit(solution)/shard_map/all_gather | solution.py:182
  389.9 205.3 %all-gather.21.cloned.1.call-start = ((), (), s32[]{:S(2)}) async-start(), calls=%async_computation.23 | async-start | bytes 1658880 | tf_op jit(solution)/shard_map/all_gather | solution.py:182
  427.8 15.0 %collective-permute-start.9 = (bf16[256,1152]{1,0:T(8,128)(2,1)S(1)}, bf16[256,1152]{1,0:T(8,128)(2,1)S(1)}, u32[]{:S(2)}, u32[]{:S(2)}) collective-permute-start(bf16[256,1152]{1,0:T(8,128)(2,1)S(1)} %convert_element_type.137), channel_id=1, source_target_pairs={{0,8},{8,16},{16,24},{24,0},{1,9},{9,17},{17,25},{25,1},{2,10},{10... | collective-permute-start | bytes 1769480 | tf_op jit(solution)/shard_map/ppermute | solution.py:26
  427.9 72.3 %collective-permute-start.11 = (bf16[256,1152]{1,0:T(8,128)(2,1)S(1)}, bf16[256,1152]{1,0:T(8,128)(2,1)}, u32[]{:S(2)}, u32[]{:S(2)}) collective-permute-start(bf16[256,1152]{1,0:T(8,128)(2,1)S(1)} %convert_element_type.137), channel_id=1, source_target_pairs={{0,24},{8,0},{16,8},{24,16},{1,25},{9,1},{17,9},{25,17},{2,26},{10... | collective-permute-start | bytes 1769480 | tf_op jit(solution)/shard_map/ppermute | solution.py:28
  442.8 57.3 %collective-permute-start.10 = (bf16[256,1152]{1,0:T(8,128)(2,1)S(1)}, bf16[256,1152]{1,0:T(8,128)(2,1)}, u32[]{:S(2)}, u32[]{:S(2)}) collective-permute-start(bf16[256,1152]{1,0:T(8,128)(2,1)S(1)} %collective-permute-done.9), channel_id=1, source_target_pairs={{0,8},{8,16},{16,24},{24,0},{1,9},{9,17},{17,25},{25,1},{2,10},{10... | collective-permute-start | bytes 1769480 | tf_op jit(solution)/shard_map/ppermute | solution.py:26
  500.1 117.8 %reduce-scatter.20.cloned.1.call-start = ((), (), s32[]{:S(2)}) async-start(), calls=%async_computation.17 | async-start | bytes 2322432 | tf_op jit(solution)/shard_map/reduce_scatter | solution.py:130
  509.5 1.4 copy-start.10
  513.4 3.2 copy-start.15
  517.4 1.1 copy-start.16
  543.6 1.3 copy-start.5
  543.9 2.9 copy-start.9
  545.0 1.8 copy-start.4
  550.8 101.4 %reduce-scatter.18.cloned.1.call-start = ((), (), s32[]{:S(2)}) async-start(), calls=%async_computation.16 | async-start | bytes 2949120 | tf_op jit(solution)/shard_map/reduce_scatter | solution.py:71
  558.1 1.8 copy-start.18
  558.1 169.3 %reduce-scatter.22.cloned.1.call-start = ((), (), s32[]{:S(2)}) async-start(), calls=%async_computation.18 | async-start | bytes 2985984 | tf_op jit(solution)/shard_map/reduce_scatter | solution.py:146
  558.2 2.8 copy-start.11
  562.7 230.2 %reduce-scatter.28.cloned.1.call-start = ((), (), s32[]{:S(2)}) async-start(), calls=%async_computation.24 | async-start | bytes 663552
  653.9 173.9 %copy-start.1 = (bf16[144,4304]{1,0:T(8,128)(2,1)S(1)}, bf16[144,4304]{1,0:T(8,128)(2,1)}, u32[]{:S(2)}) copy-start(bf16[144,4304]{1,0:T(8,128)(2,1)} %param.14) | copy-start | bytes 3718660
  655.0 170.9 %all-reduce.4.cloned.1.call-start = ((), (), s32[]{:S(2)}) async-start(), calls=%async_computation.19 | async-start | bytes 663552 | tf_op jit(solution)/shard_map/psum | solution.py:187
  (2 other events, 1.7 us)
Sparse Core Ops, SparseCore 0:
  10.8 51.4 all-gather.10
  64.4 53.5 all-gather.12
  122.2 31.3 reduce-scatter.11
  156.2 54.9 all-gather.14
  213.8 53.5 all-gather.16
  283.0 31.4 reduce-scatter.15
  318.1 71.7 reduce-scatter.23
  393.0 31.7 reduce-scatter.13
  428.5 71.5 reduce-scatter.25
  501.4 17.2 all-gather.18
  520.3 18.2 all-gather.20
  550.9 66.8 reduce-scatter.19
  620.3 31.7 reduce-scatter.17
  655.7 71.6 reduce-scatter.21
  731.1 61.7 reduce-scatter.27
  795.1 30.7 all-reduce.3
